TPU v7x, 32 devices: a whole 2x2x4 slice. The times are simulated.
32 devices in a mesh: dp: 8 (over z, y), section: 4 (over x, core).
Axes of the slice: x: 2, y: 2, z: 4, core: 2. Of those that a mesh axis runs over, the one named last changes fastest.
Arguments:
- patches: bfloat16 [64, 197, 1024], P('dp'), may hold values from -6 to 6
- ln1_gain: float32 [4, 1024], P('section'), may hold values from 0.5 to 1.5
- w_qkv: bfloat16 [4, 1024, 3072], P('section'), may hold values from -1 to 1
- w_out: bfloat16 [4, 1024, 1024], P('section'), may hold values from -0.1875 to 0.1875
- ln2_gain: float32 [4, 1024], P('section'), may hold values from 0.5 to 1.5
- w_fc1: bfloat16 [4, 1024, 2048], P('section'), may hold values from -0.1875 to 0.1875
- w_fc2: bfloat16 [4, 2048, 1024], P('section'), may hold values from -0.125 to 0.125
- final_norm_gain: float32 [1024], replicated, may hold values from 0.5 to 1.5
- w_head: bfloat16 [1024, 256], replicated, may hold values from -0.1875 to 0.1875
- online_embeddings: bfloat16 [64, 256], P('dp'), may hold values from -60 to 60
- queue: bfloat16 [32768, 256], P(('dp', 'section')), may hold values from -1 to 1, as said below
- owner: int32 [64], replicated, may hold values from 0 to 63, each once
- pointer: int32 [8], P('dp'), may hold values from 0 to 4088
Outputs:
- momentum_embeddings: bfloat16 [64, 256], P('dp')
- query_loss: float32 [64], P('dp')
- total_loss: float32 [], replicated
- new_queue: bfloat16 [32768, 256], P(('dp', 'section'))
Inputs may be any that keep to these rules, and one draw needn't show every extreme that they name: `queue`: every row has Euclidean norm below 1. Each value appears once: key j goes to group owner[j] // 8, so every group receives exactly 8 keys. `pointer`: first row of the group's shard where its new keys are written.
All inputs are finite; a program needn't handle non-finite values.
Results may differ from a plain program's by a relative error of at most 0.02.
Values may be sent and summed in bfloat16 or wider, within the bound.
No kernel may reach another device: no remote copies, remote signals or barrier semaphores. Data moves between devices by JAX's collectives and lax.ppermute only.
A program may use at most 128 MiB of HBM per device.

v0:
```python
import math
import jax
import jax.numpy as jnp
from jax import lax
from jax.sharding import PartitionSpec as P

HEADS = 16
HEAD_DIM = 64
TOKS = 197
IMG_MB = 2
contrastive_sharpness = 0.2


def from_behind(value, axis, steps):
    count = lax.axis_size(axis)
    initial, last = (max(0, -steps), min(count, count - steps))
    return lax.ppermute(value, axis, [(source, source + steps) for source in range(initial, last)])


def broadcast(value, axis, source):
    kept = jnp.where(lax.axis_index(axis) == source, value, 0).astype(value.dtype)
    return lax.psum(kept, axis)


def layer_norm(values, gain):
    center = values - jnp.mean(values, axis=-1, keepdims=True)
    spread = jnp.mean(center * center, axis=-1, keepdims=True)
    return center * lax.rsqrt(spread + 1e-06) * gain


def encoder_block(hidden, gain_one, qkv_weight, out_weight, gain_two, first_weight, second_weight):
    images = hidden.shape[0]
    width = hidden.shape[2]
    stream = hidden.astype(jnp.float32)
    normed = layer_norm(stream, gain_one).astype(jnp.bfloat16).reshape(images * TOKS, width)
    packed = jnp.dot(normed, qkv_weight, preferred_element_type=jnp.float32).astype(jnp.bfloat16)
    packed = packed.reshape(images, TOKS, 3, HEADS, HEAD_DIM)
    similarity_matrix = jnp.einsum(
        "bqhd,bkhd->bhqk", packed[:, :, 0], packed[:, :, 1], preferred_element_type=jnp.float32
    )
    similarity_matrix = similarity_matrix / math.sqrt(HEAD_DIM)
    peak = jnp.max(similarity_matrix, axis=-1, keepdims=True)
    expo = jnp.exp(similarity_matrix - peak)
    probs = (expo / jnp.sum(expo, axis=-1, keepdims=True)).astype(jnp.bfloat16)
    context = jnp.einsum(
        "bhqk,bkhd->bqhd", probs, packed[:, :, 2], preferred_element_type=jnp.float32
    )
    context = context.astype(jnp.bfloat16).reshape(images * TOKS, width)
    stream = stream + jnp.dot(context, out_weight, preferred_element_type=jnp.float32).reshape(
        images, TOKS, width
    )
    normed = layer_norm(stream, gain_two).astype(jnp.bfloat16).reshape(images * TOKS, width)
    inner = jax.nn.gelu(
        jnp.dot(normed, first_weight, preferred_element_type=jnp.float32), approximate=False
    )
    inner = inner.astype(jnp.bfloat16)
    stream = stream + jnp.dot(inner, second_weight, preferred_element_type=jnp.float32).reshape(
        images, TOKS, width
    )
    return stream.astype(jnp.bfloat16)


def key_head(class_rows, final_norm_gain, w_head):
    normed = layer_norm(class_rows.astype(jnp.float32), final_norm_gain).astype(jnp.bfloat16)
    projected = jnp.dot(normed, w_head, preferred_element_type=jnp.float32)
    scale = lax.rsqrt(1.0 + jnp.sum(projected * projected, axis=1, keepdims=True))
    return (projected * scale).astype(jnp.bfloat16)


def on_device(
    patches,
    ln1_gain,
    w_qkv,
    w_out,
    ln2_gain,
    w_fc1,
    w_fc2,
    final_norm_gain,
    w_head,
    online_embeddings,
    queue,
    owner,
    pointer,
):
    sections = lax.axis_size("section")
    section_index = lax.axis_index("section")
    group_index = lax.axis_index("dp")
    group_images = patches.shape[0]
    width = patches.shape[2]
    batch_size = IMG_MB // 2
    blocks = group_images // batch_size
    feeds = patches.reshape(blocks, batch_size, TOKS, width)

    def run_block(hidden):
        return encoder_block(
            hidden, ln1_gain[0], w_qkv[0], w_out[0], ln2_gain[0], w_fc1[0], w_fc2[0]
        )

    def keep_block(hidden):
        return hidden

    def advance(tick, carry):
        incoming, finished = carry
        fresh = lax.dynamic_index_in_dim(feeds, jnp.minimum(tick, blocks - 1), 0, keepdims=False)
        source = jnp.where(section_index == 0, fresh, incoming)
        active = jnp.logical_and(tick >= section_index, tick - section_index < blocks)
        result = lax.cond(active, run_block, keep_block, source)
        place = jnp.clip(tick - (sections - 1), 0, blocks - 1)
        stored = lax.dynamic_update_index_in_dim(finished, result[:, 0, :], place, 0)
        finished = jnp.where(tick >= sections - 1, stored, finished)
        passed = from_behind(result, "section", 1)
        return (passed, finished)

    start = (jnp.zeros_like(feeds[0]), jnp.zeros((blocks, batch_size, width), jnp.bfloat16))
    passed, finished = lax.fori_loop(0, blocks + sections - 1, advance, start)
    resident_embeddings = key_head(finished.reshape(group_images, width), final_norm_gain, w_head)
    momentum_embeddings = broadcast(resident_embeddings, "section", sections - 1)
    query_rows_full = lax.all_gather(online_embeddings, "dp", axis=0, tiled=True)
    share = queue.shape[0]
    similarity_matrix = (
        jnp.einsum("tw,fw->tf", query_rows_full, queue, preferred_element_type=jnp.float32)
        / contrastive_sharpness
    )
    local_peak = jnp.max(similarity_matrix, axis=1)
    top = lax.pmax(local_peak, ("dp", "section"))
    total = lax.psum(jnp.sum(jnp.exp(similarity_matrix - top[:, None]), axis=1), ("dp", "section"))
    negative_all = top + jnp.log(total)
    negative = lax.dynamic_slice_in_dim(negative_all, group_index * group_images, group_images, 0)
    matching_similarity = (
        jnp.sum(
            online_embeddings.astype(jnp.float32) * momentum_embeddings.astype(jnp.float32), axis=1
        )
        / contrastive_sharpness
    )
    larger = jnp.maximum(negative, matching_similarity)
    query_loss = (
        larger
        + jnp.log(jnp.exp(negative - larger) + jnp.exp(matching_similarity - larger))
        - matching_similarity
    )
    loss_sum = lax.psum(jnp.sum(query_loss), "dp")
    total_loss = loss_sum / (group_images * lax.axis_size("dp"))
    every_key = lax.all_gather(momentum_embeddings, "dp", axis=0, tiled=True)
    wanted = group_index * group_images + jnp.arange(group_images, dtype=jnp.int32)
    selector = (owner[None, :] == wanted[:, None]).astype(jnp.bfloat16)
    incoming_keys = jnp.dot(selector, every_key, preferred_element_type=jnp.float32).astype(
        jnp.bfloat16
    )
    row_place = section_index * share + jnp.arange(share, dtype=jnp.int32)
    slot_index = row_place - pointer[0]
    placing = (slot_index[:, None] == jnp.arange(group_images, dtype=jnp.int32)[None, :]).astype(
        jnp.bfloat16
    )
    written = jnp.dot(placing, incoming_keys, preferred_element_type=jnp.float32).astype(
        jnp.bfloat16
    )
    inside = jnp.logical_and(slot_index >= 0, slot_index < group_images)
    new_queue = jnp.where(inside[:, None], written, queue)
    return (momentum_embeddings, query_loss, total_loss, new_queue)


def solution(mesh):
    placed = (
        P("dp", None, None),
        P("section", None),
        P("section", None, None),
        P("section", None, None),
        P("section", None),
        P("section", None, None),
        P("section", None, None),
        P(),
        P(),
        P("dp", None),
        P(("dp", "section"), None),
        P(),
        P("dp"),
    )
    return jax.shard_map(
        on_device,
        mesh=mesh,
        in_specs=placed,
        out_specs=(P("dp", None), P("dp"), P(), P(("dp", "section"), None)),
        check_vma=False,
    )
```

profile of v0, /device:TPU:0, one launch (start us, length us, event | category | flops | bytes accessed | tf_op | source)
XLA Modules:
  0.0 522.6 jit_solution(10496831233054502232)
XLA Ops:
  6.2 320.3 %while.17 = (s32[]{:T(128)}, bf16[1,197,1024]{2,1,0:T(8,128)(2,1)S(1)}, bf16[8,1,1024]{2,1,0:T(2,128)(2,1)S(1)}, s32[]{:T(128)}, pred[]{:T(512)}, /*index=5*/bf1...) while((s32[]{:T(128)}, ...), condition=%wide.region_9.10_spmd, body=%wide.region_0.9_spmd.sunk | while | flops 3499673600 | bytes 49231128 | solution.py:115
  7.4 22.1 %conditional.2 = (bf16[1,197,1024]{2,1,0:T(8,128)(2,1)S(1)}) conditional(s32[]{:T(128)} %convert_element_type.128, bf16[1,197,1024]{2,1,0:T(8,128)(2,1)S(1)} %bitcast_select_fusion.2, (bf16[1,197,1024]{2,1,0:T(8,128)(2,1)S(1)}, f32[1,1024]{1,0:T(1,128)S(1)}, bf16[1,1024,3072]{2,1,0:T(8,128)(2,1)}, bf16[1,1024,1024]{2,1,0:T(8,128)(2,1)}, ...), branch_computations={%region_1.1_spmd, %region_2.8_spmd} | conditional | flops 3499470848 | bytes 46394252 | solution.py:107
  20.7 8.7 %fusion.40 = bf16[1,197,1024]{2,1,0:T(8,128)(2,1)S(1)} fusion(f32[1,197,1024]{2,1,0:T(8,128)S(1)} %get-tuple-element.344, bf16[1,2048,1024]{2,1,0:T(8,128)(2,1)} %get-tuple-element.295, bf16[1,1024,2048]{2,1,0:T(8,128)(2,1)} %get-tuple-element.294, f32[1024]{0:T(1024)S(1)} %bitcast.93, f32[197]{0:T(256)S(1)} %add_rsqrt_fusion, ...), kind=kOutput, calls=%fused_computation.40 | convolution fusion | flops 1679990784 | bytes 9604648 | tf_op jit(solution)/shard_map/while/body/eval_jaxpr/cond/branch_1_fun/dot_general | solution.py:57
  33.2 22.1 %conditional.2 = (bf16[1,197,1024]{2,1,0:T(8,128)(2,1)S(1)}) conditional(s32[]{:T(128)} %convert_element_type.128, bf16[1,197,1024]{2,1,0:T(8,128)(2,1)S(1)} %bitcast_select_fusion.2, (bf16[1,197,1024]{2,1,0:T(8,128)(2,1)S(1)}, f32[1,1024]{1,0:T(1,128)S(1)}, bf16[1,1024,3072]{2,1,0:T(8,128)(2,1)}, bf16[1,1024,1024]{2,1,0:T(8,128)(2,1)}, ...), branch_computations={%region_1.1_spmd, %region_2.8_spmd} | conditional | flops 3499470848 | bytes 46394252 | solution.py:107
  46.6 8.7 %fusion.40 = bf16[1,197,1024]{2,1,0:T(8,128)(2,1)S(1)} fusion(f32[1,197,1024]{2,1,0:T(8,128)S(1)} %get-tuple-element.344, bf16[1,2048,1024]{2,1,0:T(8,128)(2,1)} %get-tuple-element.295, bf16[1,1024,2048]{2,1,0:T(8,128)(2,1)} %get-tuple-element.294, f32[1024]{0:T(1024)S(1)} %bitcast.93, f32[197]{0:T(256)S(1)} %add_rsqrt_fusion, ...), kind=kOutput, calls=%fused_computation.40 | convolution fusion | flops 1679990784 | bytes 9604648 | tf_op jit(solution)/shard_map/while/body/eval_jaxpr/cond/branch_1_fun/dot_general | solution.py:57
  60.0 22.1 %conditional.2 = (bf16[1,197,1024]{2,1,0:T(8,128)(2,1)S(1)}) conditional(s32[]{:T(128)} %convert_element_type.128, bf16[1,197,1024]{2,1,0:T(8,128)(2,1)S(1)} %bitcast_select_fusion.2, (bf16[1,197,1024]{2,1,0:T(8,128)(2,1)S(1)}, f32[1,1024]{1,0:T(1,128)S(1)}, bf16[1,1024,3072]{2,1,0:T(8,128)(2,1)}, bf16[1,1024,1024]{2,1,0:T(8,128)(2,1)}, ...), branch_computations={%region_1.1_spmd, %region_2.8_spmd} | conditional | flops 3499470848 | bytes 46394252 | solution.py:107
  73.4 8.7 %fusion.40 = bf16[1,197,1024]{2,1,0:T(8,128)(2,1)S(1)} fusion(f32[1,197,1024]{2,1,0:T(8,128)S(1)} %get-tuple-element.344, bf16[1,2048,1024]{2,1,0:T(8,128)(2,1)} %get-tuple-element.295, bf16[1,1024,2048]{2,1,0:T(8,128)(2,1)} %get-tuple-element.294, f32[1024]{0:T(1024)S(1)} %bitcast.93, f32[197]{0:T(256)S(1)} %add_rsqrt_fusion, ...), kind=kOutput, calls=%fused_computation.40 | convolution fusion | flops 1679990784 | bytes 9604648 | tf_op jit(solution)/shard_map/while/body/eval_jaxpr/cond/branch_1_fun/dot_general | solution.py:57
  82.2 5.5 %collective-permute-start = (bf16[1,197,1024]{2,1,0:T(8,128)(2,1)S(1)}, bf16[1,197,1024]{2,1,0:T(8,128)(2,1)S(1)}, u32[]{:S(2)}, u32[]{:S(2)}) collective-permute-start(bf16[1,197,1024]{2,1,0:T(8,128)(2,1)S(1)} %get-tuple-element.476), channel_id=1, source_target_pairs={{0,1},{1,2},{2,3},{4,5},{5,6},{6,7},{8,9},{9,10},{10,11},{12,13},{... | collective-permute-start | bytes 1210376 | tf_op jit(solution)/shard_map/while/body/eval_jaxpr/ppermute | solution.py:17
  90.0 22.1 %conditional.2 = (bf16[1,197,1024]{2,1,0:T(8,128)(2,1)S(1)}) conditional(s32[]{:T(128)} %convert_element_type.128, bf16[1,197,1024]{2,1,0:T(8,128)(2,1)S(1)} %bitcast_select_fusion.2, (bf16[1,197,1024]{2,1,0:T(8,128)(2,1)S(1)}, f32[1,1024]{1,0:T(1,128)S(1)}, bf16[1,1024,3072]{2,1,0:T(8,128)(2,1)}, bf16[1,1024,1024]{2,1,0:T(8,128)(2,1)}, ...), branch_computations={%region_1.1_spmd, %region_2.8_spmd} | conditional | flops 3499470848 | bytes 46394252 | solution.py:107
  103.4 8.7 %fusion.40 = bf16[1,197,1024]{2,1,0:T(8,128)(2,1)S(1)} fusion(f32[1,197,1024]{2,1,0:T(8,128)S(1)} %get-tuple-element.344, bf16[1,2048,1024]{2,1,0:T(8,128)(2,1)} %get-tuple-element.295, bf16[1,1024,2048]{2,1,0:T(8,128)(2,1)} %get-tuple-element.294, f32[1024]{0:T(1024)S(1)} %bitcast.93, f32[197]{0:T(256)S(1)} %add_rsqrt_fusion, ...), kind=kOutput, calls=%fused_computation.40 | convolution fusion | flops 1679990784 | bytes 9604648 | tf_op jit(solution)/shard_map/while/body/eval_jaxpr/cond/branch_1_fun/dot_general | solution.py:57
  112.2 7.9 %collective-permute-start = (bf16[1,197,1024]{2,1,0:T(8,128)(2,1)S(1)}, bf16[1,197,1024]{2,1,0:T(8,128)(2,1)S(1)}, u32[]{:S(2)}, u32[]{:S(2)}) collective-permute-start(bf16[1,197,1024]{2,1,0:T(8,128)(2,1)S(1)} %get-tuple-element.476), channel_id=1, source_target_pairs={{0,1},{1,2},{2,3},{4,5},{5,6},{6,7},{8,9},{9,10},{10,11},{12,13},{... | collective-permute-start | bytes 1210376 | tf_op jit(solution)/shard_map/while/body/eval_jaxpr/ppermute | solution.py:17
  122.5 22.1 %conditional.2 = (bf16[1,197,1024]{2,1,0:T(8,128)(2,1)S(1)}) conditional(s32[]{:T(128)} %convert_element_type.128, bf16[1,197,1024]{2,1,0:T(8,128)(2,1)S(1)} %bitcast_select_fusion.2, (bf16[1,197,1024]{2,1,0:T(8,128)(2,1)S(1)}, f32[1,1024]{1,0:T(1,128)S(1)}, bf16[1,1024,3072]{2,1,0:T(8,128)(2,1)}, bf16[1,1024,1024]{2,1,0:T(8,128)(2,1)}, ...), branch_computations={%region_1.1_spmd, %region_2.8_spmd} | conditional | flops 3499470848 | bytes 46394252 | solution.py:107
  135.9 8.7 %fusion.40 = bf16[1,197,1024]{2,1,0:T(8,128)(2,1)S(1)} fusion(f32[1,197,1024]{2,1,0:T(8,128)S(1)} %get-tuple-element.344, bf16[1,2048,1024]{2,1,0:T(8,128)(2,1)} %get-tuple-element.295, bf16[1,1024,2048]{2,1,0:T(8,128)(2,1)} %get-tuple-element.294, f32[1024]{0:T(1024)S(1)} %bitcast.93, f32[197]{0:T(256)S(1)} %add_rsqrt_fusion, ...), kind=kOutput, calls=%fused_computation.40 | convolution fusion | flops 1679990784 | bytes 9604648 | tf_op jit(solution)/shard_map/while/body/eval_jaxpr/cond/branch_1_fun/dot_general | solution.py:57
  144.6 7.9 %collective-permute-start = (bf16[1,197,1024]{2,1,0:T(8,128)(2,1)S(1)}, bf16[1,197,1024]{2,1,0:T(8,128)(2,1)S(1)}, u32[]{:S(2)}, u32[]{:S(2)}) collective-permute-start(bf16[1,197,1024]{2,1,0:T(8,128)(2,1)S(1)} %get-tuple-element.476), channel_id=1, source_target_pairs={{0,1},{1,2},{2,3},{4,5},{5,6},{6,7},{8,9},{9,10},{10,11},{12,13},{... | collective-permute-start | bytes 1210376 | tf_op jit(solution)/shard_map/while/body/eval_jaxpr/ppermute | solution.py:17
  154.9 22.1 %conditional.2 = (bf16[1,197,1024]{2,1,0:T(8,128)(2,1)S(1)}) conditional(s32[]{:T(128)} %convert_element_type.128, bf16[1,197,1024]{2,1,0:T(8,128)(2,1)S(1)} %bitcast_select_fusion.2, (bf16[1,197,1024]{2,1,0:T(8,128)(2,1)S(1)}, f32[1,1024]{1,0:T(1,128)S(1)}, bf16[1,1024,3072]{2,1,0:T(8,128)(2,1)}, bf16[1,1024,1024]{2,1,0:T(8,128)(2,1)}, ...), branch_computations={%region_1.1_spmd, %region_2.8_spmd} | conditional | flops 3499470848 | bytes 46394252 | solution.py:107
  168.3 8.7 %fusion.40 = bf16[1,197,1024]{2,1,0:T(8,128)(2,1)S(1)} fusion(f32[1,197,1024]{2,1,0:T(8,128)S(1)} %get-tuple-element.344, bf16[1,2048,1024]{2,1,0:T(8,128)(2,1)} %get-tuple-element.295, bf16[1,1024,2048]{2,1,0:T(8,128)(2,1)} %get-tuple-element.294, f32[1024]{0:T(1024)S(1)} %bitcast.93, f32[197]{0:T(256)S(1)} %add_rsqrt_fusion, ...), kind=kOutput, calls=%fused_computation.40 | convolution fusion | flops 1679990784 | bytes 9604648 | tf_op jit(solution)/shard_map/while/body/eval_jaxpr/cond/branch_1_fun/dot_general | solution.py:57
  177.1 7.9 %collective-permute-start = (bf16[1,197,1024]{2,1,0:T(8,128)(2,1)S(1)}, bf16[1,197,1024]{2,1,0:T(8,128)(2,1)S(1)}, u32[]{:S(2)}, u32[]{:S(2)}) collective-permute-start(bf16[1,197,1024]{2,1,0:T(8,128)(2,1)S(1)} %get-tuple-element.476), channel_id=1, source_target_pairs={{0,1},{1,2},{2,3},{4,5},{5,6},{6,7},{8,9},{9,10},{10,11},{12,13},{... | collective-permute-start | bytes 1210376 | tf_op jit(solution)/shard_map/while/body/eval_jaxpr/ppermute | solution.py:17
  187.4 22.1 %conditional.2 = (bf16[1,197,1024]{2,1,0:T(8,128)(2,1)S(1)}) conditional(s32[]{:T(128)} %convert_element_type.128, bf16[1,197,1024]{2,1,0:T(8,128)(2,1)S(1)} %bitcast_select_fusion.2, (bf16[1,197,1024]{2,1,0:T(8,128)(2,1)S(1)}, f32[1,1024]{1,0:T(1,128)S(1)}, bf16[1,1024,3072]{2,1,0:T(8,128)(2,1)}, bf16[1,1024,1024]{2,1,0:T(8,128)(2,1)}, ...), branch_computations={%region_1.1_spmd, %region_2.8_spmd} | conditional | flops 3499470848 | bytes 46394252 | solution.py:107
  200.8 8.7 %fusion.40 = bf16[1,197,1024]{2,1,0:T(8,128)(2,1)S(1)} fusion(f32[1,197,1024]{2,1,0:T(8,128)S(1)} %get-tuple-element.344, bf16[1,2048,1024]{2,1,0:T(8,128)(2,1)} %get-tuple-element.295, bf16[1,1024,2048]{2,1,0:T(8,128)(2,1)} %get-tuple-element.294, f32[1024]{0:T(1024)S(1)} %bitcast.93, f32[197]{0:T(256)S(1)} %add_rsqrt_fusion, ...), kind=kOutput, calls=%fused_computation.40 | convolution fusion | flops 1679990784 | bytes 9604648 | tf_op jit(solution)/shard_map/while/body/eval_jaxpr/cond/branch_1_fun/dot_general | solution.py:57
  209.5 7.9 %collective-permute-start = (bf16[1,197,1024]{2,1,0:T(8,128)(2,1)S(1)}, bf16[1,197,1024]{2,1,0:T(8,128)(2,1)S(1)}, u32[]{:S(2)}, u32[]{:S(2)}) collective-permute-start(bf16[1,197,1024]{2,1,0:T(8,128)(2,1)S(1)} %get-tuple-element.476), channel_id=1, source_target_pairs={{0,1},{1,2},{2,3},{4,5},{5,6},{6,7},{8,9},{9,10},{10,11},{12,13},{... | collective-permute-start | bytes 1210376 | tf_op jit(solution)/shard_map/while/body/eval_jaxpr/ppermute | solution.py:17
  219.8 22.1 %conditional.2 = (bf16[1,197,1024]{2,1,0:T(8,128)(2,1)S(1)}) conditional(s32[]{:T(128)} %convert_element_type.128, bf16[1,197,1024]{2,1,0:T(8,128)(2,1)S(1)} %bitcast_select_fusion.2, (bf16[1,197,1024]{2,1,0:T(8,128)(2,1)S(1)}, f32[1,1024]{1,0:T(1,128)S(1)}, bf16[1,1024,3072]{2,1,0:T(8,128)(2,1)}, bf16[1,1024,1024]{2,1,0:T(8,128)(2,1)}, ...), branch_computations={%region_1.1_spmd, %region_2.8_spmd} | conditional | flops 3499470848 | bytes 46394252 | solution.py:107
  233.2 8.7 %fusion.40 = bf16[1,197,1024]{2,1,0:T(8,128)(2,1)S(1)} fusion(f32[1,197,1024]{2,1,0:T(8,128)S(1)} %get-tuple-element.344, bf16[1,2048,1024]{2,1,0:T(8,128)(2,1)} %get-tuple-element.295, bf16[1,1024,2048]{2,1,0:T(8,128)(2,1)} %get-tuple-element.294, f32[1024]{0:T(1024)S(1)} %bitcast.93, f32[197]{0:T(256)S(1)} %add_rsqrt_fusion, ...), kind=kOutput, calls=%fused_computation.40 | convolution fusion | flops 1679990784 | bytes 9604648 | tf_op jit(solution)/shard_map/while/body/eval_jaxpr/cond/branch_1_fun/dot_general | solution.py:57
  242.0 7.9 %collective-permute-start = (bf16[1,197,1024]{2,1,0:T(8,128)(2,1)S(1)}, bf16[1,197,1024]{2,1,0:T(8,128)(2,1)S(1)}, u32[]{:S(2)}, u32[]{:S(2)}) collective-permute-start(bf16[1,197,1024]{2,1,0:T(8,128)(2,1)S(1)} %get-tuple-element.476), channel_id=1, source_target_pairs={{0,1},{1,2},{2,3},{4,5},{5,6},{6,7},{8,9},{9,10},{10,11},{12,13},{... | collective-permute-start | bytes 1210376 | tf_op jit(solution)/shard_map/while/body/eval_jaxpr/ppermute | solution.py:17
  252.3 30.1 %collective-permute-start = (bf16[1,197,1024]{2,1,0:T(8,128)(2,1)S(1)}, bf16[1,197,1024]{2,1,0:T(8,128)(2,1)S(1)}, u32[]{:S(2)}, u32[]{:S(2)}) collective-permute-start(bf16[1,197,1024]{2,1,0:T(8,128)(2,1)S(1)} %get-tuple-element.476), channel_id=1, source_target_pairs={{0,1},{1,2},{2,3},{4,5},{5,6},{6,7},{8,9},{9,10},{10,11},{12,13},{... | collective-permute-start | bytes 1210376 | tf_op jit(solution)/shard_map/while/body/eval_jaxpr/ppermute | solution.py:17
  284.8 7.9 %collective-permute-start = (bf16[1,197,1024]{2,1,0:T(8,128)(2,1)S(1)}, bf16[1,197,1024]{2,1,0:T(8,128)(2,1)S(1)}, u32[]{:S(2)}, u32[]{:S(2)}) collective-permute-start(bf16[1,197,1024]{2,1,0:T(8,128)(2,1)S(1)} %get-tuple-element.476), channel_id=1, source_target_pairs={{0,1},{1,2},{2,3},{4,5},{5,6},{6,7},{8,9},{9,10},{10,11},{12,13},{... | collective-permute-start | bytes 1210376 | tf_op jit(solution)/shard_map/while/body/eval_jaxpr/ppermute | solution.py:17
  295.1 30.1 %collective-permute-start = (bf16[1,197,1024]{2,1,0:T(8,128)(2,1)S(1)}, bf16[1,197,1024]{2,1,0:T(8,128)(2,1)S(1)}, u32[]{:S(2)}, u32[]{:S(2)}) collective-permute-start(bf16[1,197,1024]{2,1,0:T(8,128)(2,1)S(1)} %get-tuple-element.476), channel_id=1, source_target_pairs={{0,1},{1,2},{2,3},{4,5},{5,6},{6,7},{8,9},{9,10},{10,11},{12,13},{... | collective-permute-start | bytes 1210376 | tf_op jit(solution)/shard_map/while/body/eval_jaxpr/ppermute | solution.py:17
  327.3 24.5 %psum.21 = bf16[8,256]{1,0:T(8,128)(2,1)S(1)} all-reduce(bf16[8,256]{1,0:T(8,128)(2,1)S(1)} %fusion.136), channel_id=1, replica_groups=mesh['dp'=8,'section'=4] {'section'}, use_global_device_ids=true, to_apply=%region_13.14 | all-reduce | flops 2048 | bytes 8192 | tf_op jit(solution)/shard_map/psum | solution.py:22
  351.8 32.6 %all_gather.7 = bf16[64,256]{1,0:T(8,128)(2,1)S(1)} all-gather(bf16[8,256]{1,0:T(8,128)(2,1)S(1)} %psum.21), channel_id=1, replica_groups=mesh['dp'=8,'section'=4] {'dp'}, dimensions={0}, use_global_device_ids=true | all-gather | bytes 36864 | tf_op jit(solution)/shard_map/all_gather | solution.py:143
  386.5 30.6 %all_gather.6 = bf16[64,256]{1,0:T(8,128)(2,1)S(1)} all-gather(bf16[8,256]{1,0:T(8,128)(2,1)S(1)} %copy-done.4), channel_id=1, replica_groups=mesh['dp'=8,'section'=4] {'dp'}, dimensions={0}, use_global_device_ids=true | all-gather | bytes 36864 | tf_op jit(solution)/shard_map/all_gather | solution.py:118
  417.5 38.5 %pmax.7 = f32[64]{0:T(128)S(1)} all-reduce(f32[64]{0:T(128)S(1)} %get-tuple-element.347), channel_id=1, replica_groups=mesh['dp'=8,'section'=4] {'dp','section'}, use_global_device_ids=true, to_apply=%region_15.16 | all-reduce | flops 64 | bytes 512 | tf_op jit(solution)/shard_map/pmax | solution.py:125
  456.3 41.6 %psum.22 = f32[64]{0:T(128)S(1)} all-reduce(f32[64]{0:T(128)S(1)} %exponential_reduce_fusion), channel_id=1, replica_groups=mesh['dp'=8,'section'=4] {'dp','section'}, use_global_device_ids=true, to_apply=%region_17.18 | all-reduce | flops 64 | bytes 512 | tf_op jit(solution)/shard_map/psum | solution.py:126
  499.1 21.7 %psum.23 = f32[]{:T(128)} all-reduce(f32[]{:T(128)} %get-tuple-element.339), channel_id=1, replica_groups=mesh['dp'=8,'section'=4] {'dp'}, use_global_device_ids=true, to_apply=%region_20.21 | all-reduce | flops 1 | bytes 8 | tf_op jit(solution)/shard_map/psum | solution.py:141
  (194 shorter events, 145.8 us)
Async XLA Ops:
  0.6 326.3 %copy-start = (bf16[1024,256]{1,0:T(8,128)(2,1)S(1)}, bf16[1024,256]{1,0:T(8,128)(2,1)}, u32[]{:S(2)}) copy-start(bf16[1024,256]{1,0:T(8,128)(2,1)} %param.25) | copy-start | bytes 1572868
  0.7 5.5 %copy-start.6 = (f32[1,1024]{1,0:T(1,128)S(1)}, f32[1,1024]{1,0:T(1,128)}, u32[]{:S(2)}) copy-start(f32[1,1024]{1,0:T(1,128)} %param.18) | copy-start | bytes 12292
  0.7 5.5 %copy-start.7 = (f32[1,1024]{1,0:T(1,128)S(1)}, f32[1,1024]{1,0:T(1,128)}, u32[]{:S(2)}) copy-start(f32[1,1024]{1,0:T(1,128)} %param.21) | copy-start | bytes 12292
  6.2 320.7 %copy-start.8 = (f32[1024]{0:T(1024)S(1)}, f32[1024]{0:T(1024)}, u32[]{:S(2)}) copy-start(f32[1024]{0:T(1024)} %param.24) | copy-start | bytes 12292
  6.2 378.9 %copy-start.2 = (bf16[1024,256]{1,0:T(8,128)(2,1)S(1)}, bf16[1024,256]{1,0:T(8,128)(2,1)}, u32[]{:S(2)}) copy-start(bf16[1024,256]{1,0:T(8,128)(2,1)} %param.27) | copy-start | bytes 1572868
  6.2 378.9 %copy-start.5 = (s32[64]{0:T(128)S(1)}, s32[64]{0:T(128)}, u32[]{:S(2)}) copy-start(s32[64]{0:T(128)} %param.28) | copy-start | bytes 772
  18.2 1.6 copy-start.1
  29.5 2.7 collective-permute-start
  44.0 1.6 copy-start.1
  55.3 3.7 collective-permute-start
  70.9 1.6 copy-start.1
  82.2 6.8 %collective-permute-start = (bf16[1,197,1024]{2,1,0:T(8,128)(2,1)S(1)}, bf16[1,197,1024]{2,1,0:T(8,128)(2,1)S(1)}, u32[]{:S(2)}, u32[]{:S(2)}) collective-permute-start(bf16[1,197,1024]{2,1,0:T(8,128)(2,1)S(1)} %get-tuple-element.476), channel_id=1, source_target_pairs={{0,1},{1,2},{2,3},{4,5},{5,6},{6,7},{8,9},{9,10},{10,11},{12,13},{... | collective-permute-start | bytes 1210376 | tf_op jit(solution)/shard_map/while/body/eval_jaxpr/ppermute | solution.py:17
  100.9 1.6 copy-start.1
  112.2 9.3 %collective-permute-start = (bf16[1,197,1024]{2,1,0:T(8,128)(2,1)S(1)}, bf16[1,197,1024]{2,1,0:T(8,128)(2,1)S(1)}, u32[]{:S(2)}, u32[]{:S(2)}) collective-permute-start(bf16[1,197,1024]{2,1,0:T(8,128)(2,1)S(1)} %get-tuple-element.476), channel_id=1, source_target_pairs={{0,1},{1,2},{2,3},{4,5},{5,6},{6,7},{8,9},{9,10},{10,11},{12,13},{... | collective-permute-start | bytes 1210376 | tf_op jit(solution)/shard_map/while/body/eval_jaxpr/ppermute | solution.py:17
  133.3 1.6 copy-start.1
  144.6 9.3 %collective-permute-start = (bf16[1,197,1024]{2,1,0:T(8,128)(2,1)S(1)}, bf16[1,197,1024]{2,1,0:T(8,128)(2,1)S(1)}, u32[]{:S(2)}, u32[]{:S(2)}) collective-permute-start(bf16[1,197,1024]{2,1,0:T(8,128)(2,1)S(1)} %get-tuple-element.476), channel_id=1, source_target_pairs={{0,1},{1,2},{2,3},{4,5},{5,6},{6,7},{8,9},{9,10},{10,11},{12,13},{... | collective-permute-start | bytes 1210376 | tf_op jit(solution)/shard_map/while/body/eval_jaxpr/ppermute | solution.py:17
  165.8 1.6 copy-start.1
  177.1 9.3 %collective-permute-start = (bf16[1,197,1024]{2,1,0:T(8,128)(2,1)S(1)}, bf16[1,197,1024]{2,1,0:T(8,128)(2,1)S(1)}, u32[]{:S(2)}, u32[]{:S(2)}) collective-permute-start(bf16[1,197,1024]{2,1,0:T(8,128)(2,1)S(1)} %get-tuple-element.476), channel_id=1, source_target_pairs={{0,1},{1,2},{2,3},{4,5},{5,6},{6,7},{8,9},{9,10},{10,11},{12,13},{... | collective-permute-start | bytes 1210376 | tf_op jit(solution)/shard_map/while/body/eval_jaxpr/ppermute | solution.py:17
  198.2 1.6 copy-start.1
  209.5 9.3 %collective-permute-start = (bf16[1,197,1024]{2,1,0:T(8,128)(2,1)S(1)}, bf16[1,197,1024]{2,1,0:T(8,128)(2,1)S(1)}, u32[]{:S(2)}, u32[]{:S(2)}) collective-permute-start(bf16[1,197,1024]{2,1,0:T(8,128)(2,1)S(1)} %get-tuple-element.476), channel_id=1, source_target_pairs={{0,1},{1,2},{2,3},{4,5},{5,6},{6,7},{8,9},{9,10},{10,11},{12,13},{... | collective-permute-start | bytes 1210376 | tf_op jit(solution)/shard_map/while/body/eval_jaxpr/ppermute | solution.py:17
  230.7 1.6 copy-start.1
  242.0 9.3 %collective-permute-start = (bf16[1,197,1024]{2,1,0:T(8,128)(2,1)S(1)}, bf16[1,197,1024]{2,1,0:T(8,128)(2,1)S(1)}, u32[]{:S(2)}, u32[]{:S(2)}) collective-permute-start(bf16[1,197,1024]{2,1,0:T(8,128)(2,1)S(1)} %get-tuple-element.476), channel_id=1, source_target_pairs={{0,1},{1,2},{2,3},{4,5},{5,6},{6,7},{8,9},{9,10},{10,11},{12,13},{... | collective-permute-start | bytes 1210376 | tf_op jit(solution)/shard_map/while/body/eval_jaxpr/ppermute | solution.py:17
  252.3 31.4 %collective-permute-start = (bf16[1,197,1024]{2,1,0:T(8,128)(2,1)S(1)}, bf16[1,197,1024]{2,1,0:T(8,128)(2,1)S(1)}, u32[]{:S(2)}, u32[]{:S(2)}) collective-permute-start(bf16[1,197,1024]{2,1,0:T(8,128)(2,1)S(1)} %get-tuple-element.476), channel_id=1, source_target_pairs={{0,1},{1,2},{2,3},{4,5},{5,6},{6,7},{8,9},{9,10},{10,11},{12,13},{... | collective-permute-start | bytes 1210376 | tf_op jit(solution)/shard_map/while/body/eval_jaxpr/ppermute | solution.py:17
  284.8 9.3 %collective-permute-start = (bf16[1,197,1024]{2,1,0:T(8,128)(2,1)S(1)}, bf16[1,197,1024]{2,1,0:T(8,128)(2,1)S(1)}, u32[]{:S(2)}, u32[]{:S(2)}) collective-permute-start(bf16[1,197,1024]{2,1,0:T(8,128)(2,1)S(1)} %get-tuple-element.476), channel_id=1, source_target_pairs={{0,1},{1,2},{2,3},{4,5},{5,6},{6,7},{8,9},{9,10},{10,11},{12,13},{... | collective-permute-start | bytes 1210376 | tf_op jit(solution)/shard_map/while/body/eval_jaxpr/ppermute | solution.py:17
  295.1 31.4 %collective-permute-start = (bf16[1,197,1024]{2,1,0:T(8,128)(2,1)S(1)}, bf16[1,197,1024]{2,1,0:T(8,128)(2,1)S(1)}, u32[]{:S(2)}, u32[]{:S(2)}) collective-permute-start(bf16[1,197,1024]{2,1,0:T(8,128)(2,1)S(1)} %get-tuple-element.476), channel_id=1, source_target_pairs={{0,1},{1,2},{2,3},{4,5},{5,6},{6,7},{8,9},{9,10},{10,11},{12,13},{... | collective-permute-start | bytes 1210376 | tf_op jit(solution)/shard_map/while/body/eval_jaxpr/ppermute | solution.py:17
  326.5 59.9 %copy-start.4 = (bf16[8,256]{1,0:T(8,128)(2,1)S(1)}, bf16[8,256]{1,0:T(8,128)(2,1)}, u32[]{:S(2)}) copy-start(bf16[8,256]{1,0:T(8,128)(2,1)} %param.26) | copy-start | bytes 12292
  351.8 169.6 %copy-start.3 = (bf16[8,256]{1,0:T(8,128)(2,1)}, bf16[8,256]{1,0:T(8,128)(2,1)S(1)}, u32[]{:S(2)}) copy-start(bf16[8,256]{1,0:T(8,128)(2,1)S(1)} %psum.21) | copy-start | bytes 12292
where the time goes:
time: 524 us; the launch traced here: 523 us
  blocking collectives  190 us (36%)
  matrix products  130 us (25%)
  starting transfers between devices  117 us (22%)
  other arithmetic  40.6 us (8%)
  local copies, waits for them, and re-layouts  27.6 us (5%)
  waiting for transfers between devices  14.3 us (3%)
    ppermute x11, starting transfers between devices, from_behind(): lax.ppermute(value, axis, [(source, source + steps) for source in range(i...  117 us
    dot_general x8, matrix products, encoder_block(): jnp.dot(inner, second_weight, preferred_element_type=jnp.float32)  70 us
    dot_general x8, matrix products, encoder_block(): jnp.dot(normed, qkv_weight, preferred_element_type=jnp.float32)  43.2 us
    psum x1, blocking collectives, on_device(): lax.psum(jnp.sum(jnp.exp(similarity_matrix - top[:, None]), axis=1), ('dp...  41.6 us
    pmax x1, blocking collectives, on_device(): top = lax.pmax(local_peak, ('dp', 'section'))  38.5 us
    all_gather x1, blocking collectives, on_device(): every_key = lax.all_gather(momentum_embeddings, 'dp', axis=0, tiled=True)  32.6 us
    all_gather x1, blocking collectives, on_device(): lax.all_gather(online_embeddings, 'dp', axis=0, tiled=True)  30.6 us
    psum x1, blocking collectives, broadcast(): return lax.psum(kept, axis)  24.5 us
  transfers between devices with their start and end apart: 11, of which 11 were waited for; matrix products, arithmetic and copies ran while one was open for 0% of the time, Pallas kernels for 0%

commit v1 on v0

--- a/solution.py
+++ b/solution.py
@@ -123,7 +123,10 @@
     )
     local_peak = jnp.max(similarity_matrix, axis=1)
     top = lax.pmax(local_peak, ("dp", "section"))
-    total = lax.psum(jnp.sum(jnp.exp(similarity_matrix - top[:, None]), axis=1), ("dp", "section"))
+    total = lax.psum(
+        lax.psum(jnp.sum(jnp.exp(similarity_matrix - top[:, None]), axis=1), axis_name="section"),
+        "dp",
+    )
     negative_all = top + jnp.log(total)
     negative = lax.dynamic_slice_in_dim(negative_all, group_index * group_images, group_images, 0)
     matching_similarity = (

time: 524 us -> 505 us (0.964)
  blocking collectives: 190 us -> 170 us
    psum x1 -> x2, blocking collectives: 41.6 us -> 26 us  [the longest x1 19.4 us: on_device(): lax.psum(lax.psum(jnp.sum(jnp.exp(similarity_matrix - top[:, None]), axis...]
where the time goes in v1:
time: 505 us; the launch traced here: 503 us
  blocking collectives  170 us (34%)
  matrix products  130 us (26%)
  starting transfers between devices  117 us (23%)
  other arithmetic  40.6 us (8%)
  local copies, waits for them, and re-layouts  27.6 us (5%)
  waiting for transfers between devices  14.3 us (3%)
    ppermute x11, starting transfers between devices, from_behind(): lax.ppermute(value, axis, [(source, source + steps) for source in range(i...  117 us
    dot_general x8, matrix products, encoder_block(): jnp.dot(inner, second_weight, preferred_element_type=jnp.float32)  70 us
    dot_general x8, matrix products, encoder_block(): jnp.dot(normed, qkv_weight, preferred_element_type=jnp.float32)  43.2 us
    pmax x1, blocking collectives, on_device(): top = lax.pmax(local_peak, ('dp', 'section'))  38.5 us
    all_gather x1, blocking collectives, on_device(): every_key = lax.all_gather(momentum_embeddings, 'dp', axis=0, tiled=True)  32.4 us
    all_gather x1, blocking collectives, on_device(): lax.all_gather(online_embeddings, 'dp', axis=0, tiled=True)  30.6 us
    psum x1, blocking collectives, broadcast(): return lax.psum(kept, axis)  24.5 us
    sub x8, other arithmetic, encoder_block(): expo = jnp.exp(similarity_matrix - peak)  21.6 us
  transfers between devices with their start and end apart: 11, of which 11 were waited for; matrix products, arithmetic and copies ran while one was open for 0% of the time, Pallas kernels for 0%

profile of v1, /device:TPU:0, one launch (start us, length us, event | category | flops | bytes accessed | tf_op | source)
XLA Modules:
  0.0 502.8 jit_solution(5158841526508921717)
XLA Ops:
  6.2 320.3 %while.17 = (s32[]{:T(128)}, bf16[1,197,1024]{2,1,0:T(8,128)(2,1)S(1)}, bf16[8,1,1024]{2,1,0:T(2,128)(2,1)S(1)}, s32[]{:T(128)}, pred[]{:T(512)}, /*index=5*/bf1...) while((s32[]{:T(128)}, ...), condition=%wide.region_9.10_spmd, body=%wide.region_0.9_spmd.sunk | while | flops 3499673600 | bytes 49231128 | solution.py:115
  7.4 22.1 %conditional.2 = (bf16[1,197,1024]{2,1,0:T(8,128)(2,1)S(1)}) conditional(s32[]{:T(128)} %convert_element_type.128, bf16[1,197,1024]{2,1,0:T(8,128)(2,1)S(1)} %bitcast_select_fusion.2, (bf16[1,197,1024]{2,1,0:T(8,128)(2,1)S(1)}, f32[1,1024]{1,0:T(1,128)S(1)}, bf16[1,1024,3072]{2,1,0:T(8,128)(2,1)}, bf16[1,1024,1024]{2,1,0:T(8,128)(2,1)}, ...), branch_computations={%region_1.1_spmd, %region_2.8_spmd} | conditional | flops 3499470848 | bytes 46394252 | solution.py:107
  20.7 8.7 %fusion.40 = bf16[1,197,1024]{2,1,0:T(8,128)(2,1)S(1)} fusion(f32[1,197,1024]{2,1,0:T(8,128)S(1)} %get-tuple-element.344, bf16[1,2048,1024]{2,1,0:T(8,128)(2,1)} %get-tuple-element.295, bf16[1,1024,2048]{2,1,0:T(8,128)(2,1)} %get-tuple-element.294, f32[1024]{0:T(1024)S(1)} %bitcast.93, f32[197]{0:T(256)S(1)} %add_rsqrt_fusion, ...), kind=kOutput, calls=%fused_computation.40 | convolution fusion | flops 1679990784 | bytes 9604648 | tf_op jit(solution)/shard_map/while/body/eval_jaxpr/cond/branch_1_fun/dot_general | solution.py:57
  33.2 22.1 %conditional.2 = (bf16[1,197,1024]{2,1,0:T(8,128)(2,1)S(1)}) conditional(s32[]{:T(128)} %convert_element_type.128, bf16[1,197,1024]{2,1,0:T(8,128)(2,1)S(1)} %bitcast_select_fusion.2, (bf16[1,197,1024]{2,1,0:T(8,128)(2,1)S(1)}, f32[1,1024]{1,0:T(1,128)S(1)}, bf16[1,1024,3072]{2,1,0:T(8,128)(2,1)}, bf16[1,1024,1024]{2,1,0:T(8,128)(2,1)}, ...), branch_computations={%region_1.1_spmd, %region_2.8_spmd} | conditional | flops 3499470848 | bytes 46394252 | solution.py:107
  46.6 8.7 %fusion.40 = bf16[1,197,1024]{2,1,0:T(8,128)(2,1)S(1)} fusion(f32[1,197,1024]{2,1,0:T(8,128)S(1)} %get-tuple-element.344, bf16[1,2048,1024]{2,1,0:T(8,128)(2,1)} %get-tuple-element.295, bf16[1,1024,2048]{2,1,0:T(8,128)(2,1)} %get-tuple-element.294, f32[1024]{0:T(1024)S(1)} %bitcast.93, f32[197]{0:T(256)S(1)} %add_rsqrt_fusion, ...), kind=kOutput, calls=%fused_computation.40 | convolution fusion | flops 1679990784 | bytes 9604648 | tf_op jit(solution)/shard_map/while/body/eval_jaxpr/cond/branch_1_fun/dot_general | solution.py:57
  60.0 22.1 %conditional.2 = (bf16[1,197,1024]{2,1,0:T(8,128)(2,1)S(1)}) conditional(s32[]{:T(128)} %convert_element_type.128, bf16[1,197,1024]{2,1,0:T(8,128)(2,1)S(1)} %bitcast_select_fusion.2, (bf16[1,197,1024]{2,1,0:T(8,128)(2,1)S(1)}, f32[1,1024]{1,0:T(1,128)S(1)}, bf16[1,1024,3072]{2,1,0:T(8,128)(2,1)}, bf16[1,1024,1024]{2,1,0:T(8,128)(2,1)}, ...), branch_computations={%region_1.1_spmd, %region_2.8_spmd} | conditional | flops 3499470848 | bytes 46394252 | solution.py:107
  73.4 8.7 %fusion.40 = bf16[1,197,1024]{2,1,0:T(8,128)(2,1)S(1)} fusion(f32[1,197,1024]{2,1,0:T(8,128)S(1)} %get-tuple-element.344, bf16[1,2048,1024]{2,1,0:T(8,128)(2,1)} %get-tuple-element.295, bf16[1,1024,2048]{2,1,0:T(8,128)(2,1)} %get-tuple-element.294, f32[1024]{0:T(1024)S(1)} %bitcast.93, f32[197]{0:T(256)S(1)} %add_rsqrt_fusion, ...), kind=kOutput, calls=%fused_computation.40 | convolution fusion | flops 1679990784 | bytes 9604648 | tf_op jit(solution)/shard_map/while/body/eval_jaxpr/cond/branch_1_fun/dot_general | solution.py:57
  90.0 22.1 %conditional.2 = (bf16[1,197,1024]{2,1,0:T(8,128)(2,1)S(1)}) conditional(s32[]{:T(128)} %convert_element_type.128, bf16[1,197,1024]{2,1,0:T(8,128)(2,1)S(1)} %bitcast_select_fusion.2, (bf16[1,197,1024]{2,1,0:T(8,128)(2,1)S(1)}, f32[1,1024]{1,0:T(1,128)S(1)}, bf16[1,1024,3072]{2,1,0:T(8,128)(2,1)}, bf16[1,1024,1024]{2,1,0:T(8,128)(2,1)}, ...), branch_computations={%region_1.1_spmd, %region_2.8_spmd} | conditional | flops 3499470848 | bytes 46394252 | solution.py:107
  103.4 8.7 %fusion.40 = bf16[1,197,1024]{2,1,0:T(8,128)(2,1)S(1)} fusion(f32[1,197,1024]{2,1,0:T(8,128)S(1)} %get-tuple-element.344, bf16[1,2048,1024]{2,1,0:T(8,128)(2,1)} %get-tuple-element.295, bf16[1,1024,2048]{2,1,0:T(8,128)(2,1)} %get-tuple-element.294, f32[1024]{0:T(1024)S(1)} %bitcast.93, f32[197]{0:T(256)S(1)} %add_rsqrt_fusion, ...), kind=kOutput, calls=%fused_computation.40 | convolution fusion | flops 1679990784 | bytes 9604648 | tf_op jit(solution)/shard_map/while/body/eval_jaxpr/cond/branch_1_fun/dot_general | solution.py:57
  112.2 7.9 %collective-permute-start = (bf16[1,197,1024]{2,1,0:T(8,128)(2,1)S(1)}, bf16[1,197,1024]{2,1,0:T(8,128)(2,1)S(1)}, u32[]{:S(2)}, u32[]{:S(2)}) collective-permute-start(bf16[1,197,1024]{2,1,0:T(8,128)(2,1)S(1)} %get-tuple-element.476), channel_id=1, source_target_pairs={{0,1},{1,2},{2,3},{4,5},{5,6},{6,7},{8,9},{9,10},{10,11},{12,13},{... | collective-permute-start | bytes 1210376 | tf_op jit(solution)/shard_map/while/body/eval_jaxpr/ppermute | solution.py:17
  122.5 22.1 %conditional.2 = (bf16[1,197,1024]{2,1,0:T(8,128)(2,1)S(1)}) conditional(s32[]{:T(128)} %convert_element_type.128, bf16[1,197,1024]{2,1,0:T(8,128)(2,1)S(1)} %bitcast_select_fusion.2, (bf16[1,197,1024]{2,1,0:T(8,128)(2,1)S(1)}, f32[1,1024]{1,0:T(1,128)S(1)}, bf16[1,1024,3072]{2,1,0:T(8,128)(2,1)}, bf16[1,1024,1024]{2,1,0:T(8,128)(2,1)}, ...), branch_computations={%region_1.1_spmd, %region_2.8_spmd} | conditional | flops 3499470848 | bytes 46394252 | solution.py:107
  135.9 8.7 %fusion.40 = bf16[1,197,1024]{2,1,0:T(8,128)(2,1)S(1)} fusion(f32[1,197,1024]{2,1,0:T(8,128)S(1)} %get-tuple-element.344, bf16[1,2048,1024]{2,1,0:T(8,128)(2,1)} %get-tuple-element.295, bf16[1,1024,2048]{2,1,0:T(8,128)(2,1)} %get-tuple-element.294, f32[1024]{0:T(1024)S(1)} %bitcast.93, f32[197]{0:T(256)S(1)} %add_rsqrt_fusion, ...), kind=kOutput, calls=%fused_computation.40 | convolution fusion | flops 1679990784 | bytes 9604648 | tf_op jit(solution)/shard_map/while/body/eval_jaxpr/cond/branch_1_fun/dot_general | solution.py:57
  144.6 7.9 %collective-permute-start = (bf16[1,197,1024]{2,1,0:T(8,128)(2,1)S(1)}, bf16[1,197,1024]{2,1,0:T(8,128)(2,1)S(1)}, u32[]{:S(2)}, u32[]{:S(2)}) collective-permute-start(bf16[1,197,1024]{2,1,0:T(8,128)(2,1)S(1)} %get-tuple-element.476), channel_id=1, source_target_pairs={{0,1},{1,2},{2,3},{4,5},{5,6},{6,7},{8,9},{9,10},{10,11},{12,13},{... | collective-permute-start | bytes 1210376 | tf_op jit(solution)/shard_map/while/body/eval_jaxpr/ppermute | solution.py:17
  154.9 22.1 %conditional.2 = (bf16[1,197,1024]{2,1,0:T(8,128)(2,1)S(1)}) conditional(s32[]{:T(128)} %convert_element_type.128, bf16[1,197,1024]{2,1,0:T(8,128)(2,1)S(1)} %bitcast_select_fusion.2, (bf16[1,197,1024]{2,1,0:T(8,128)(2,1)S(1)}, f32[1,1024]{1,0:T(1,128)S(1)}, bf16[1,1024,3072]{2,1,0:T(8,128)(2,1)}, bf16[1,1024,1024]{2,1,0:T(8,128)(2,1)}, ...), branch_computations={%region_1.1_spmd, %region_2.8_spmd} | conditional | flops 3499470848 | bytes 46394252 | solution.py:107
  168.3 8.7 %fusion.40 = bf16[1,197,1024]{2,1,0:T(8,128)(2,1)S(1)} fusion(f32[1,197,1024]{2,1,0:T(8,128)S(1)} %get-tuple-element.344, bf16[1,2048,1024]{2,1,0:T(8,128)(2,1)} %get-tuple-element.295, bf16[1,1024,2048]{2,1,0:T(8,128)(2,1)} %get-tuple-element.294, f32[1024]{0:T(1024)S(1)} %bitcast.93, f32[197]{0:T(256)S(1)} %add_rsqrt_fusion, ...), kind=kOutput, calls=%fused_computation.40 | convolution fusion | flops 1679990784 | bytes 9604648 | tf_op jit(solution)/shard_map/while/body/eval_jaxpr/cond/branch_1_fun/dot_general | solution.py:57
  177.1 7.9 %collective-permute-start = (bf16[1,197,1024]{2,1,0:T(8,128)(2,1)S(1)}, bf16[1,197,1024]{2,1,0:T(8,128)(2,1)S(1)}, u32[]{:S(2)}, u32[]{:S(2)}) collective-permute-start(bf16[1,197,1024]{2,1,0:T(8,128)(2,1)S(1)} %get-tuple-element.476), channel_id=1, source_target_pairs={{0,1},{1,2},{2,3},{4,5},{5,6},{6,7},{8,9},{9,10},{10,11},{12,13},{... | collective-permute-start | bytes 1210376 | tf_op jit(solution)/shard_map/while/body/eval_jaxpr/ppermute | solution.py:17
  187.4 22.1 %conditional.2 = (bf16[1,197,1024]{2,1,0:T(8,128)(2,1)S(1)}) conditional(s32[]{:T(128)} %convert_element_type.128, bf16[1,197,1024]{2,1,0:T(8,128)(2,1)S(1)} %bitcast_select_fusion.2, (bf16[1,197,1024]{2,1,0:T(8,128)(2,1)S(1)}, f32[1,1024]{1,0:T(1,128)S(1)}, bf16[1,1024,3072]{2,1,0:T(8,128)(2,1)}, bf16[1,1024,1024]{2,1,0:T(8,128)(2,1)}, ...), branch_computations={%region_1.1_spmd, %region_2.8_spmd} | conditional | flops 3499470848 | bytes 46394252 | solution.py:107
  200.8 8.7 %fusion.40 = bf16[1,197,1024]{2,1,0:T(8,128)(2,1)S(1)} fusion(f32[1,197,1024]{2,1,0:T(8,128)S(1)} %get-tuple-element.344, bf16[1,2048,1024]{2,1,0:T(8,128)(2,1)} %get-tuple-element.295, bf16[1,1024,2048]{2,1,0:T(8,128)(2,1)} %get-tuple-element.294, f32[1024]{0:T(1024)S(1)} %bitcast.93, f32[197]{0:T(256)S(1)} %add_rsqrt_fusion, ...), kind=kOutput, calls=%fused_computation.40 | convolution fusion | flops 1679990784 | bytes 9604648 | tf_op jit(solution)/shard_map/while/body/eval_jaxpr/cond/branch_1_fun/dot_general | solution.py:57
  209.5 7.9 %collective-permute-start = (bf16[1,197,1024]{2,1,0:T(8,128)(2,1)S(1)}, bf16[1,197,1024]{2,1,0:T(8,128)(2,1)S(1)}, u32[]{:S(2)}, u32[]{:S(2)}) collective-permute-start(bf16[1,197,1024]{2,1,0:T(8,128)(2,1)S(1)} %get-tuple-element.476), channel_id=1, source_target_pairs={{0,1},{1,2},{2,3},{4,5},{5,6},{6,7},{8,9},{9,10},{10,11},{12,13},{... | collective-permute-start | bytes 1210376 | tf_op jit(solution)/shard_map/while/body/eval_jaxpr/ppermute | solution.py:17
  219.8 22.1 %conditional.2 = (bf16[1,197,1024]{2,1,0:T(8,128)(2,1)S(1)}) conditional(s32[]{:T(128)} %convert_element_type.128, bf16[1,197,1024]{2,1,0:T(8,128)(2,1)S(1)} %bitcast_select_fusion.2, (bf16[1,197,1024]{2,1,0:T(8,128)(2,1)S(1)}, f32[1,1024]{1,0:T(1,128)S(1)}, bf16[1,1024,3072]{2,1,0:T(8,128)(2,1)}, bf16[1,1024,1024]{2,1,0:T(8,128)(2,1)}, ...), branch_computations={%region_1.1_spmd, %region_2.8_spmd} | conditional | flops 3499470848 | bytes 46394252 | solution.py:107
  233.2 8.7 %fusion.40 = bf16[1,197,1024]{2,1,0:T(8,128)(2,1)S(1)} fusion(f32[1,197,1024]{2,1,0:T(8,128)S(1)} %get-tuple-element.344, bf16[1,2048,1024]{2,1,0:T(8,128)(2,1)} %get-tuple-element.295, bf16[1,1024,2048]{2,1,0:T(8,128)(2,1)} %get-tuple-element.294, f32[1024]{0:T(1024)S(1)} %bitcast.93, f32[197]{0:T(256)S(1)} %add_rsqrt_fusion, ...), kind=kOutput, calls=%fused_computation.40 | convolution fusion | flops 1679990784 | bytes 9604648 | tf_op jit(solution)/shard_map/while/body/eval_jaxpr/cond/branch_1_fun/dot_general | solution.py:57
  242.0 7.9 %collective-permute-start = (bf16[1,197,1024]{2,1,0:T(8,128)(2,1)S(1)}, bf16[1,197,1024]{2,1,0:T(8,128)(2,1)S(1)}, u32[]{:S(2)}, u32[]{:S(2)}) collective-permute-start(bf16[1,197,1024]{2,1,0:T(8,128)(2,1)S(1)} %get-tuple-element.476), channel_id=1, source_target_pairs={{0,1},{1,2},{2,3},{4,5},{5,6},{6,7},{8,9},{9,10},{10,11},{12,13},{... | collective-permute-start | bytes 1210376 | tf_op jit(solution)/shard_map/while/body/eval_jaxpr/ppermute | solution.py:17
  252.3 30.1 %collective-permute-start = (bf16[1,197,1024]{2,1,0:T(8,128)(2,1)S(1)}, bf16[1,197,1024]{2,1,0:T(8,128)(2,1)S(1)}, u32[]{:S(2)}, u32[]{:S(2)}) collective-permute-start(bf16[1,197,1024]{2,1,0:T(8,128)(2,1)S(1)} %get-tuple-element.476), channel_id=1, source_target_pairs={{0,1},{1,2},{2,3},{4,5},{5,6},{6,7},{8,9},{9,10},{10,11},{12,13},{... | collective-permute-start | bytes 1210376 | tf_op jit(solution)/shard_map/while/body/eval_jaxpr/ppermute | solution.py:17
  284.8 7.9 %collective-permute-start = (bf16[1,197,1024]{2,1,0:T(8,128)(2,1)S(1)}, bf16[1,197,1024]{2,1,0:T(8,128)(2,1)S(1)}, u32[]{:S(2)}, u32[]{:S(2)}) collective-permute-start(bf16[1,197,1024]{2,1,0:T(8,128)(2,1)S(1)} %get-tuple-element.476), channel_id=1, source_target_pairs={{0,1},{1,2},{2,3},{4,5},{5,6},{6,7},{8,9},{9,10},{10,11},{12,13},{... | collective-permute-start | bytes 1210376 | tf_op jit(solution)/shard_map/while/body/eval_jaxpr/ppermute | solution.py:17
  295.1 30.1 %collective-permute-start = (bf16[1,197,1024]{2,1,0:T(8,128)(2,1)S(1)}, bf16[1,197,1024]{2,1,0:T(8,128)(2,1)S(1)}, u32[]{:S(2)}, u32[]{:S(2)}) collective-permute-start(bf16[1,197,1024]{2,1,0:T(8,128)(2,1)S(1)} %get-tuple-element.476), channel_id=1, source_target_pairs={{0,1},{1,2},{2,3},{4,5},{5,6},{6,7},{8,9},{9,10},{10,11},{12,13},{... | collective-permute-start | bytes 1210376 | tf_op jit(solution)/shard_map/while/body/eval_jaxpr/ppermute | solution.py:17
  327.3 24.5 %psum.28 = bf16[8,256]{1,0:T(8,128)(2,1)S(1)} all-reduce(bf16[8,256]{1,0:T(8,128)(2,1)S(1)} %fusion.136), channel_id=1, replica_groups=mesh['dp'=8,'section'=4] {'section'}, use_global_device_ids=true, to_apply=%region_13.14 | all-reduce | flops 2048 | bytes 8192 | tf_op jit(solution)/shard_map/psum | solution.py:22
  351.8 32.4 %all_gather.7 = bf16[64,256]{1,0:T(8,128)(2,1)S(1)} all-gather(bf16[8,256]{1,0:T(8,128)(2,1)S(1)} %psum.28), channel_id=1, replica_groups=mesh['dp'=8,'section'=4] {'dp'}, dimensions={0}, use_global_device_ids=true | all-gather | bytes 36864 | tf_op jit(solution)/shard_map/all_gather | solution.py:146
  386.3 30.6 %all_gather.6 = bf16[64,256]{1,0:T(8,128)(2,1)S(1)} all-gather(bf16[8,256]{1,0:T(8,128)(2,1)S(1)} %copy-done.4), channel_id=1, replica_groups=mesh['dp'=8,'section'=4] {'dp'}, dimensions={0}, use_global_device_ids=true | all-gather | bytes 36864 | tf_op jit(solution)/shard_map/all_gather | solution.py:118
  417.3 38.5 %pmax.7 = f32[64]{0:T(128)S(1)} all-reduce(f32[64]{0:T(128)S(1)} %get-tuple-element.347), channel_id=1, replica_groups=mesh['dp'=8,'section'=4] {'dp','section'}, use_global_device_ids=true, to_apply=%region_15.16 | all-reduce | flops 64 | bytes 512 | tf_op jit(solution)/shard_map/pmax | solution.py:125
  456.1 6.6 %psum.29 = f32[64]{0:T(128)S(1)} all-reduce(f32[64]{0:T(128)S(1)} %exponential_reduce_fusion), channel_id=1, replica_groups=mesh['dp'=8,'section'=4] {'section'}, use_global_device_ids=true, to_apply=%region_17.18 | all-reduce | flops 64 | bytes 512 | tf_op jit(solution)/shard_map/psum | solution.py:127
  462.7 19.4 %psum.30 = f32[64]{0:T(128)S(1)} all-reduce(f32[64]{0:T(128)S(1)} %psum.29), channel_id=1, replica_groups=mesh['dp'=8,'section'=4] {'dp'}, use_global_device_ids=true, to_apply=%region_18.19 | all-reduce | flops 64 | bytes 512 | tf_op jit(solution)/shard_map/psum | solution.py:126
  483.3 17.7 %psum.31 = f32[]{:T(128)} all-reduce(f32[]{:T(128)} %get-tuple-element.339), channel_id=1, replica_groups=mesh['dp'=8,'section'=4] {'dp'}, use_global_device_ids=true, to_apply=%region_21.22 | all-reduce | flops 1 | bytes 8 | tf_op jit(solution)/shard_map/psum | solution.py:144
  (195 shorter events, 151.3 us)
Async XLA Ops:
  0.6 326.3 %copy-start = (bf16[1024,256]{1,0:T(8,128)(2,1)S(1)}, bf16[1024,256]{1,0:T(8,128)(2,1)}, u32[]{:S(2)}) copy-start(bf16[1024,256]{1,0:T(8,128)(2,1)} %param.25) | copy-start | bytes 1572868
  0.7 5.5 %copy-start.6 = (f32[1,1024]{1,0:T(1,128)S(1)}, f32[1,1024]{1,0:T(1,128)}, u32[]{:S(2)}) copy-start(f32[1,1024]{1,0:T(1,128)} %param.18) | copy-start | bytes 12292
  0.7 5.5 %copy-start.7 = (f32[1,1024]{1,0:T(1,128)S(1)}, f32[1,1024]{1,0:T(1,128)}, u32[]{:S(2)}) copy-start(f32[1,1024]{1,0:T(1,128)} %param.21) | copy-start | bytes 12292
  6.2 320.7 %copy-start.8 = (f32[1024]{0:T(1024)S(1)}, f32[1024]{0:T(1024)}, u32[]{:S(2)}) copy-start(f32[1024]{0:T(1024)} %param.24) | copy-start | bytes 12292
  6.2 378.7 %copy-start.2 = (bf16[1024,256]{1,0:T(8,128)(2,1)S(1)}, bf16[1024,256]{1,0:T(8,128)(2,1)}, u32[]{:S(2)}) copy-start(bf16[1024,256]{1,0:T(8,128)(2,1)} %param.27) | copy-start | bytes 1572868
  6.2 378.7 %copy-start.5 = (s32[64]{0:T(128)S(1)}, s32[64]{0:T(128)}, u32[]{:S(2)}) copy-start(s32[64]{0:T(128)} %param.28) | copy-start | bytes 772
  18.2 1.6 copy-start.1
  29.5 2.7 collective-permute-start
  44.0 1.6 copy-start.1
  55.3 3.7 collective-permute-start
  70.9 1.6 copy-start.1
  82.2 6.8 %collective-permute-start = (bf16[1,197,1024]{2,1,0:T(8,128)(2,1)S(1)}, bf16[1,197,1024]{2,1,0:T(8,128)(2,1)S(1)}, u32[]{:S(2)}, u32[]{:S(2)}) collective-permute-start(bf16[1,197,1024]{2,1,0:T(8,128)(2,1)S(1)} %get-tuple-element.476), channel_id=1, source_target_pairs={{0,1},{1,2},{2,3},{4,5},{5,6},{6,7},{8,9},{9,10},{10,11},{12,13},{... | collective-permute-start | bytes 1210376 | tf_op jit(solution)/shard_map/while/body/eval_jaxpr/ppermute | solution.py:17
  100.9 1.6 copy-start.1
  112.2 9.3 %collective-permute-start = (bf16[1,197,1024]{2,1,0:T(8,128)(2,1)S(1)}, bf16[1,197,1024]{2,1,0:T(8,128)(2,1)S(1)}, u32[]{:S(2)}, u32[]{:S(2)}) collective-permute-start(bf16[1,197,1024]{2,1,0:T(8,128)(2,1)S(1)} %get-tuple-element.476), channel_id=1, source_target_pairs={{0,1},{1,2},{2,3},{4,5},{5,6},{6,7},{8,9},{9,10},{10,11},{12,13},{... | collective-permute-start | bytes 1210376 | tf_op jit(solution)/shard_map/while/body/eval_jaxpr/ppermute | solution.py:17
  133.3 1.6 copy-start.1
  144.6 9.3 %collective-permute-start = (bf16[1,197,1024]{2,1,0:T(8,128)(2,1)S(1)}, bf16[1,197,1024]{2,1,0:T(8,128)(2,1)S(1)}, u32[]{:S(2)}, u32[]{:S(2)}) collective-permute-start(bf16[1,197,1024]{2,1,0:T(8,128)(2,1)S(1)} %get-tuple-element.476), channel_id=1, source_target_pairs={{0,1},{1,2},{2,3},{4,5},{5,6},{6,7},{8,9},{9,10},{10,11},{12,13},{... | collective-permute-start | bytes 1210376 | tf_op jit(solution)/shard_map/while/body/eval_jaxpr/ppermute | solution.py:17
  165.8 1.6 copy-start.1
  177.1 9.3 %collective-permute-start = (bf16[1,197,1024]{2,1,0:T(8,128)(2,1)S(1)}, bf16[1,197,1024]{2,1,0:T(8,128)(2,1)S(1)}, u32[]{:S(2)}, u32[]{:S(2)}) collective-permute-start(bf16[1,197,1024]{2,1,0:T(8,128)(2,1)S(1)} %get-tuple-element.476), channel_id=1, source_target_pairs={{0,1},{1,2},{2,3},{4,5},{5,6},{6,7},{8,9},{9,10},{10,11},{12,13},{... | collective-permute-start | bytes 1210376 | tf_op jit(solution)/shard_map/while/body/eval_jaxpr/ppermute | solution.py:17
  198.2 1.6 copy-start.1
  209.5 9.3 %collective-permute-start = (bf16[1,197,1024]{2,1,0:T(8,128)(2,1)S(1)}, bf16[1,197,1024]{2,1,0:T(8,128)(2,1)S(1)}, u32[]{:S(2)}, u32[]{:S(2)}) collective-permute-start(bf16[1,197,1024]{2,1,0:T(8,128)(2,1)S(1)} %get-tuple-element.476), channel_id=1, source_target_pairs={{0,1},{1,2},{2,3},{4,5},{5,6},{6,7},{8,9},{9,10},{10,11},{12,13},{... | collective-permute-start | bytes 1210376 | tf_op jit(solution)/shard_map/while/body/eval_jaxpr/ppermute | solution.py:17
  230.7 1.6 copy-start.1
  242.0 9.3 %collective-permute-start = (bf16[1,197,1024]{2,1,0:T(8,128)(2,1)S(1)}, bf16[1,197,1024]{2,1,0:T(8,128)(2,1)S(1)}, u32[]{:S(2)}, u32[]{:S(2)}) collective-permute-start(bf16[1,197,1024]{2,1,0:T(8,128)(2,1)S(1)} %get-tuple-element.476), channel_id=1, source_target_pairs={{0,1},{1,2},{2,3},{4,5},{5,6},{6,7},{8,9},{9,10},{10,11},{12,13},{... | collective-permute-start | bytes 1210376 | tf_op jit(solution)/shard_map/while/body/eval_jaxpr/ppermute | solution.py:17
  252.3 31.4 %collective-permute-start = (bf16[1,197,1024]{2,1,0:T(8,128)(2,1)S(1)}, bf16[1,197,1024]{2,1,0:T(8,128)(2,1)S(1)}, u32[]{:S(2)}, u32[]{:S(2)}) collective-permute-start(bf16[1,197,1024]{2,1,0:T(8,128)(2,1)S(1)} %get-tuple-element.476), channel_id=1, source_target_pairs={{0,1},{1,2},{2,3},{4,5},{5,6},{6,7},{8,9},{9,10},{10,11},{12,13},{... | collective-permute-start | bytes 1210376 | tf_op jit(solution)/shard_map/while/body/eval_jaxpr/ppermute | solution.py:17
  284.8 9.3 %collective-permute-start = (bf16[1,197,1024]{2,1,0:T(8,128)(2,1)S(1)}, bf16[1,197,1024]{2,1,0:T(8,128)(2,1)S(1)}, u32[]{:S(2)}, u32[]{:S(2)}) collective-permute-start(bf16[1,197,1024]{2,1,0:T(8,128)(2,1)S(1)} %get-tuple-element.476), channel_id=1, source_target_pairs={{0,1},{1,2},{2,3},{4,5},{5,6},{6,7},{8,9},{9,10},{10,11},{12,13},{... | collective-permute-start | bytes 1210376 | tf_op jit(solution)/shard_map/while/body/eval_jaxpr/ppermute | solution.py:17
  295.1 31.4 %collective-permute-start = (bf16[1,197,1024]{2,1,0:T(8,128)(2,1)S(1)}, bf16[1,197,1024]{2,1,0:T(8,128)(2,1)S(1)}, u32[]{:S(2)}, u32[]{:S(2)}) collective-permute-start(bf16[1,197,1024]{2,1,0:T(8,128)(2,1)S(1)} %get-tuple-element.476), channel_id=1, source_target_pairs={{0,1},{1,2},{2,3},{4,5},{5,6},{6,7},{8,9},{9,10},{10,11},{12,13},{... | collective-permute-start | bytes 1210376 | tf_op jit(solution)/shard_map/while/body/eval_jaxpr/ppermute | solution.py:17
  326.5 59.7 %copy-start.4 = (bf16[8,256]{1,0:T(8,128)(2,1)S(1)}, bf16[8,256]{1,0:T(8,128)(2,1)}, u32[]{:S(2)}) copy-start(bf16[8,256]{1,0:T(8,128)(2,1)} %param.26) | copy-start | bytes 12292
  351.8 149.9 %copy-start.3 = (bf16[8,256]{1,0:T(8,128)(2,1)}, bf16[8,256]{1,0:T(8,128)(2,1)S(1)}, u32[]{:S(2)}) copy-start(bf16[8,256]{1,0:T(8,128)(2,1)S(1)} %psum.28) | copy-start | bytes 12292
